TPU v7x, 32 devices: a whole 2x2x4 slice. The times are simulated.
32 devices in a mesh: tm: 4 (over y, x), space: 8 (over z, core).
Axes of the slice: x: 2, y: 2, z: 4, core: 2. Of those that a mesh axis runs over, the one named last changes fastest.
Arguments:
- state: float32 [4, 6, 8, 128, 128], P('tm', None, None, 'space'), may hold values from -6 to 6
- multiplier: float32 [4, 6, 8, 128, 128], P('tm', None, None, 'space'), may hold values from -6 to 6
- members: bfloat16 [4, 40, 6, 8, 128, 128], P('tm', None, None, None, 'space'), may hold values from -6 to 6
- static_var: float32 [4, 6, 8, 128, 128], P('tm', None, None, 'space'), may hold values from 0.1 to 1
- courant: float32 [4, 2, 8, 128, 128], P('tm', None, None, 'space'), may hold values from -0.45 to 0.45
- coupling: float32 [8, 6, 6], replicated, may hold values from -2 to 2
- loc_offsets: int32 [9], replicated, may hold values from -8 to 8, as said below
Outputs:
- first_row: float32 [4, 6, 8, 128, 128], P('tm', None, None, 'space')
Inputs may be any that keep to these rules, and one draw needn't show every extreme that they name: `loc_offsets`: both -8 and 8 occur among the offsets.
All inputs are finite; a program needn't handle non-finite values.
Results may differ from a plain program's by a relative error of at most 0.0013.
Values may be sent and summed in bfloat16 or wider, within the bound.
No kernel may reach another device: no remote copies, remote signals or barrier semaphores. Data moves between devices by JAX's collectives and lax.ppermute only.
A program may use at most 128 MiB of HBM per device.

v0:
```python
import jax
import jax.numpy as jnp
from jax import lax
from jax.sharding import PartitionSpec as P


def passed_along(block, axis, distance):
    devices = range(lax.axis_size(axis))
    route = [(i - distance, i) for i in devices if i - distance in devices]
    return lax.ppermute(block, axis, route)


def padded_2(array, sides, width):
    for axis, dim in sides:
        size, length = (lax.axis_size(axis), array.shape[dim])
        up = [(i, (i + 1) % size) for i in range(size)]
        down = [(j, i) for i, j in up]
        last = lax.slice_in_dim(array, length - width, length, axis=dim)
        leading = lax.slice_in_dim(array, 0, width, axis=dim)
        before = lax.ppermute(last, axis, up)
        after = lax.ppermute(leading, axis, down)
        array = jnp.concatenate([before, array, after], axis=dim)
    return array


def tangent_step(padded, winds, coupling):
    center = padded[:, :, 1:-1]
    west_cells = padded[:, :, :-2]
    east_cells = padded[:, :, 2:]
    zero_row = jnp.zeros_like(center[..., :1])
    south_cells = jnp.concatenate([zero_row, center[..., :-1]], axis=-1)
    north_cells = jnp.concatenate([center[..., 1:], zero_row], axis=-1)
    courant_x = winds[0]
    courant_y = winds[1]
    advection = jnp.maximum(courant_x, 0.0) * (center - west_cells)
    advection = advection + jnp.minimum(courant_x, 0.0) * (east_cells - center)
    advection = advection + jnp.maximum(courant_y, 0.0) * (center - south_cells)
    advection = advection + jnp.minimum(courant_y, 0.0) * (north_cells - center)
    coupling_term = jnp.einsum("lvw,wlxy->vlxy", coupling, center, precision=lax.Precision.HIGHEST)
    return center - advection + coupling_term


def per_device(state, multiplier, members, static_var, courant, coupling, loc_offsets):
    own_state = state[0]
    lagrange = multiplier[0]
    ensemble = members[0]
    variance = static_var[0]
    own_winds = courant[0]
    span_cells = ensemble.shape[3]
    radius = span_cells // 2
    member_count = ensemble.shape[0]
    stencil_count = loc_offsets.shape[0]
    weights = jnp.exp(-0.5 * (loc_offsets.astype(jnp.float32) / radius) ** 2)
    earlier = passed_along(own_state, "tm", 1)
    padded_state = padded_2(earlier, (("space", 2),), 2)
    padded_winds = padded_2(own_winds.astype(jnp.bfloat16), (("space", 2),), 1).astype(
        own_winds.dtype
    )
    halfway = tangent_step(padded_state, padded_winds, coupling)
    propagated = tangent_step(halfway, own_winds, coupling)
    products = (ensemble.astype(jnp.float32) * lagrange[None]).astype(jnp.bfloat16)
    padded_products = padded_2(products, (("space", 3),), radius)
    smoothed = jnp.zeros(ensemble.shape, jnp.float32)
    for index in range(stencil_count):
        offset_start = radius + loc_offsets[index]
        shifted = lax.dynamic_slice_in_dim(padded_products, offset_start, span_cells, 3)
        smoothed = smoothed + weights[index] * shifted.astype(jnp.float32)
    total = jnp.sum(ensemble.astype(jnp.float32) * smoothed, axis=0)
    localized = total / (member_count - 1)
    result = 0.5 * variance * lagrange + 0.5 * localized + own_state - propagated
    return result[None]


def solution(mesh):
    return jax.shard_map(
        per_device,
        mesh=mesh,
        in_specs=(
            P("tm", None, None, "space", None),
            P("tm", None, None, "space", None),
            P("tm", None, None, None, "space", None),
            P("tm", None, None, "space", None),
            P("tm", None, None, "space", None),
            P(),
            P(),
        ),
        out_specs=P("tm", None, None, "space", None),
        check_vma=False,
    )
```

profile of v0, /device:TPU:0, one launch (start us, length us, event | category | flops | bytes accessed | tf_op | source)
XLA Modules:
  0.0 172.9 jit_solution(944658474341322933)
XLA Ops:
  0.0 0.0 copy-start
  0.0 5.4 %fusion = bf16[40,6,8,16,128]{4,3,2,1,0:T(8,128)(2,1)S(1)} fusion(bf16[1,40,6,8,16,128]{5,4,3,2,1,0:T(8,128)(2,1)} %param.9, f32[6,8,16,128]{3,2,1,0:T(8,128)} %bitcast.81), kind=kLoop, calls=%fused_computation.2 | loop fusion | flops 11796480 | bytes 16121856 | tf_op jit(solution)/shard_map/convert_element_type | solution.py:61
  5.4 0.0 copy-start.1
  5.4 3.0 %copy-done.1 = bf16[40,6,8,16,128]{4,3,2,1,0:T(8,128)(2,1)} copy-done((bf16[40,6,8,16,128]{4,3,2,1,0:T(8,128)(2,1)}, bf16[40,6,8,16,128]{4,3,2,1,0:T(8,128)(2,1)S(1)}, u32[]{:S(2)}) %copy-start.1) | copy-done | bytes 7864344
  8.4 4.1 %fusion.26 = (bf16[40,6,8,8,128]{4,3,2,1,0:T(8,128)(2,1)}, bf16[40,6,8,8,128]{4,3,2,1,0:T(8,128)(2,1)}) fusion(bf16[40,6,8,16,128]{4,3,2,1,0:T(8,128)(2,1)S(1)} %fusion), kind=kLoop, calls=%fused_computation.49 | loop fusion | bytes 15728640 | tf_op jit(solution)/shard_map/slice | solution.py:18
  12.5 0.5 collective-permute-start
  13.0 4.0 %collective-permute-start.1 = (bf16[40,6,8,8,128]{4,3,2,1,0:T(8,128)(2,1)}, bf16[40,6,8,8,128]{4,3,2,1,0:T(8,128)(2,1)}, u32[]{:S(2)}, u32[]{:S(2)}) collective-permute-start(bf16[40,6,8,8,128]{4,3,2,1,0:T(8,128)(2,1)} %get-tuple-element.6), channel_id=1, source_target_pairs={{1,0},{2,1},{3,2},{4,3},{5,4},{6,5},{7,6},{0,7},{9,8},{10,9},{11,1... | collective-permute-start | bytes 11796488 | tf_op jit(solution)/shard_map/ppermute | solution.py:21
  17.0 0.0 copy-done.3
  17.0 0.2 copy.48
  17.3 3.9 %collective-permute-start.2 = (f32[6,8,16,128]{3,0,2,1:T(8,128)S(1)}, f32[6,8,16,128]{3,0,2,1:T(8,128)S(1)}, u32[]{:S(2)}, u32[]{:S(2)}) collective-permute-start(f32[6,8,16,128]{3,0,2,1:T(8,128)S(1)} %bitcast.82), channel_id=1, source_target_pairs={{0,8},{8,16},{16,24},{1,9},{9,17},{17,25},{2,10},{10,18},{18,26},{... | collective-permute-start | bytes 1179656 | tf_op jit(solution)/shard_map/ppermute | solution.py:10
  21.3 0.1 collective-permute-start.5
  21.3 3.5 %collective-permute-start.6 = (bf16[2,8,1,128]{3,2,1,0:T(2,128)(2,1)S(1)}, bf16[2,8,1,128]{3,2,1,0:T(2,128)(2,1)S(1)}, u32[]{:S(2)}, u32[]{:S(2)}) collective-permute-start(bf16[2,8,1,128]{3,2,1,0:T(2,128)(2,1)S(1)} %get-tuple-element.22), channel_id=1, source_target_pairs={{1,0},{2,1},{3,2},{4,3},{5,4},{6,5},{7,6},{0,7},{9,8},{10,9},{11,1... | collective-permute-start | bytes 12296 | tf_op jit(solution)/shard_map/ppermute | solution.py:21
  24.9 0.7 maximum_bitcast_fusion.3
  25.5 0.7 fusion.32
  26.2 0.7 fusion.31
  38.3 62.0 %collective-permute-done.5 = bf16[2,8,1,128]{3,2,1,0:T(2,128)(2,1)S(1)} collective-permute-done((bf16[2,8,1,128]{3,2,1,0:T(2,128)(2,1)S(1)}, bf16[2,8,1,128]{3,2,1,0:T(2,128)(2,1)S(1)}, u32[]{:S(2)}, u32[]{:S(2)}) %collective-permute-start.5) | collective-permute-done | bytes 4128 | tf_op jit(solution)/shard_map/ppermute | solution.py:20
  100.3 0.5 collective-permute-done.6
  100.8 0.0 collective-permute-done.2
  100.9 2.0 %collective-permute-start.3 = (f32[6,8,2,128]{3,0,2,1:T(8,128)S(1)}, f32[6,8,2,128]{3,0,2,1:T(8,128)S(1)}, u32[]{:S(2)}, u32[]{:S(2)}) collective-permute-start(f32[6,8,2,128]{3,0,2,1:T(8,128)S(1)} %get-tuple-element.12), channel_id=1, source_target_pairs={{0,1},{1,2},{2,3},{3,4},{4,5},{5,6},{6,7},{7,0},{8,9},{9,10},{10,1... | collective-permute-start | bytes 147464 | tf_op jit(solution)/shard_map/ppermute | solution.py:20
  102.9 2.0 %collective-permute-start.4 = (f32[6,8,2,128]{3,0,2,1:T(8,128)S(1)}, f32[6,8,2,128]{3,0,2,1:T(8,128)S(1)}, u32[]{:S(2)}, u32[]{:S(2)}) collective-permute-start(f32[6,8,2,128]{3,0,2,1:T(8,128)S(1)} %get-tuple-element.11), channel_id=1, source_target_pairs={{1,0},{2,1},{3,2},{4,3},{5,4},{6,5},{7,6},{0,7},{9,8},{10,9},{11,1... | collective-permute-start | bytes 147464 | tf_op jit(solution)/shard_map/ppermute | solution.py:21
  105.0 1.7 collective-permute-done.3
  106.7 0.2 collective-permute-done.4
  106.9 0.2 fusion.27
  107.1 1.0 fusion.7
  108.1 0.2 fusion.28
  108.3 0.0 collective-permute-done
  108.3 0.0 collective-permute-done.1
  108.3 0.0 copy-done.2
  108.4 10.7 %pad_maximum_fusion = bf16[40,6,8,32,128]{4,3,2,1,0:T(8,128)(2,1)} fusion(bf16[40,6,8,8,128]{4,3,2,1,0:T(8,128)(2,1)} %collective-permute-done.1, bf16[40,6,8,16,128]{4,3,2,1,0:T(8,128)(2,1)S(1)} %copy-done.2, bf16[40,6,8,8,128]{4,3,2,1,0:T(8,128)(2,1)} %collective-permute-done), kind=kLoop, calls=%fused_computation.4 | loop fusion | flops 47185920 | bytes 31457280 | tf_op jit(solution)/shard_map/concatenate | solution.py:22
  119.0 50.3 %fusion.1 = f32[6,8,16,128]{3,2,1,0:T(8,128)S(1)} fusion(bf16[1,40,6,8,16,128]{5,4,3,2,1,0:T(8,128)(2,1)} %param.9, bf16[40,6,8,32,128]{4,3,2,1,0:T(8,128)(2,1)} %pad_maximum_fusion, s32[]{:T(128)S(6)} %select_n.35, f32[]{:T(128)} %bitcast.29, s32[]{:T(128)S(6)} %select_n.34, f32[]{:T(128)} %bitcast.26, s32[]{:T(128)S(6)} %select_n.33, f32[]{:T(128)} %bitcast.23, ...), kind=kLoop, calls=%fused_computation.3 | loop fusion | flops 113934336 | bytes 79036488 | tf_op jit(solution)/shard_map/reduce_sum | solution.py:68
  169.3 2.8 %fusion.16 = f32[1,6,8,16,128]{4,1,3,2,0:T(8,128)S(1)} fusion(f32[6,8,18,128]{3,0,2,1:T(8,128)S(1)} %fusion.7, f32[6,8,16,128]{3,2,1,0:T(8,128)S(1)} %fusion.1, f32[1,6,8,16,128]{4,3,2,1,0:T(8,128)S(1)} %copy-done.4, f32[1,6,8,16,128]{4,3,2,1,0:T(8,128)} %param.10, f32[6,8,16,127]{3,0,2,1:T(8,128)S(1)} %get-tuple-element.10, ...), kind=kOutput, calls=%fused_computation.24 | convolution fusion | flops 8945664 | bytes 5464064 | tf_op jit(solution)/shard_map/lvw,wlxy->vlxy/dot_general | solution.py:39
  172.1 0.8 copy.22
  (18 shorter events, 0.2 us)
Async XLA Ops:
  0.0 107.1 %copy-start = (f32[8,6,6]{2,0,1:T(8,128)S(1)}, f32[8,6,6]{2,0,1:T(8,128)}, u32[]{:S(2)}) copy-start(f32[8,6,6]{2,0,1:T(8,128)} %param.12) | copy-start | bytes 3460
  0.0 17.0 %copy-start.3 = (f32[1,6,8,16,128]{4,3,2,1,0:T(8,128)S(1)}, f32[1,6,8,16,128]{4,3,2,1,0:T(8,128)}, u32[]{:S(2)}) copy-start(f32[1,6,8,16,128]{4,3,2,1,0:T(8,128)} %param.7) | copy-start | bytes 1179652
  0.0 25.5 %copy-start.6 = (s32[9]{0:T(128)S(1)}, s32[9]{0:T(128)}, u32[]{:S(2)}) copy-start(s32[9]{0:T(128)} %param.13) | copy-start | bytes 112
  5.4 3.0 %copy-start.1 = (bf16[40,6,8,16,128]{4,3,2,1,0:T(8,128)(2,1)}, bf16[40,6,8,16,128]{4,3,2,1,0:T(8,128)(2,1)S(1)}, u32[]{:S(2)}) copy-start(bf16[40,6,8,16,128]{4,3,2,1,0:T(8,128)(2,1)S(1)} %fusion) | copy-start | bytes 23592964
  8.4 12.8 %copy-start.5 = (f32[1,2,8,16,128]{4,3,2,1,0:T(8,128)S(1)}, f32[1,2,8,16,128]{4,3,2,1,0:T(8,128)}, u32[]{:S(2)}) copy-start(f32[1,2,8,16,128]{4,3,2,1,0:T(8,128)} %param.11) | copy-start | bytes 393220
  12.5 95.8 %collective-permute-start = (bf16[40,6,8,8,128]{4,3,2,1,0:T(8,128)(2,1)}, bf16[40,6,8,8,128]{4,3,2,1,0:T(8,128)(2,1)}, u32[]{:S(2)}, u32[]{:S(2)}) collective-permute-start(bf16[40,6,8,8,128]{4,3,2,1,0:T(8,128)(2,1)} %get-tuple-element.5), channel_id=1, source_target_pairs={{0,1},{1,2},{2,3},{3,4},{4,5},{5,6},{6,7},{7,0},{8,9},{9,10},{10,1... | collective-permute-start | bytes 11796488 | tf_op jit(solution)/shard_map/ppermute | solution.py:20
  13.0 95.3 %collective-permute-start.1 = (bf16[40,6,8,8,128]{4,3,2,1,0:T(8,128)(2,1)}, bf16[40,6,8,8,128]{4,3,2,1,0:T(8,128)(2,1)}, u32[]{:S(2)}, u32[]{:S(2)}) collective-permute-start(bf16[40,6,8,8,128]{4,3,2,1,0:T(8,128)(2,1)} %get-tuple-element.6), channel_id=1, source_target_pairs={{1,0},{2,1},{3,2},{4,3},{5,4},{6,5},{7,6},{0,7},{9,8},{10,9},{11,1... | collective-permute-start | bytes 11796488 | tf_op jit(solution)/shard_map/ppermute | solution.py:21
  17.3 83.6 %collective-permute-start.2 = (f32[6,8,16,128]{3,0,2,1:T(8,128)S(1)}, f32[6,8,16,128]{3,0,2,1:T(8,128)S(1)}, u32[]{:S(2)}, u32[]{:S(2)}) collective-permute-start(f32[6,8,16,128]{3,0,2,1:T(8,128)S(1)} %bitcast.82), channel_id=1, source_target_pairs={{0,8},{8,16},{16,24},{1,9},{9,17},{17,25},{2,10},{10,18},{18,26},{... | collective-permute-start | bytes 1179656 | tf_op jit(solution)/shard_map/ppermute | solution.py:10
  21.3 79.1 %collective-permute-start.5 = (bf16[2,8,1,128]{3,2,1,0:T(2,128)(2,1)S(1)}, bf16[2,8,1,128]{3,2,1,0:T(2,128)(2,1)S(1)}, u32[]{:S(2)}, u32[]{:S(2)}) collective-permute-start(bf16[2,8,1,128]{3,2,1,0:T(2,128)(2,1)S(1)} %get-tuple-element.21), channel_id=1, source_target_pairs={{0,1},{1,2},{2,3},{3,4},{4,5},{5,6},{6,7},{7,0},{8,9},{9,10},{10,1... | collective-permute-start | bytes 12296 | tf_op jit(solution)/shard_map/ppermute | solution.py:20
  21.3 79.5 %collective-permute-start.6 = (bf16[2,8,1,128]{3,2,1,0:T(2,128)(2,1)S(1)}, bf16[2,8,1,128]{3,2,1,0:T(2,128)(2,1)S(1)}, u32[]{:S(2)}, u32[]{:S(2)}) collective-permute-start(bf16[2,8,1,128]{3,2,1,0:T(2,128)(2,1)S(1)} %get-tuple-element.22), channel_id=1, source_target_pairs={{1,0},{2,1},{3,2},{4,3},{5,4},{6,5},{7,6},{0,7},{9,8},{10,9},{11,1... | collective-permute-start | bytes 12296 | tf_op jit(solution)/shard_map/ppermute | solution.py:21
  38.3 70.0 %copy-start.2 = (bf16[40,6,8,16,128]{4,3,2,1,0:T(8,128)(2,1)S(1)}, bf16[40,6,8,16,128]{4,3,2,1,0:T(8,128)(2,1)}, u32[]{:S(2)}) copy-start(bf16[40,6,8,16,128]{4,3,2,1,0:T(8,128)(2,1)} %copy-done.1) | copy-start | bytes 23592964
  100.9 5.8 %collective-permute-start.3 = (f32[6,8,2,128]{3,0,2,1:T(8,128)S(1)}, f32[6,8,2,128]{3,0,2,1:T(8,128)S(1)}, u32[]{:S(2)}, u32[]{:S(2)}) collective-permute-start(f32[6,8,2,128]{3,0,2,1:T(8,128)S(1)} %get-tuple-element.12), channel_id=1, source_target_pairs={{0,1},{1,2},{2,3},{3,4},{4,5},{5,6},{6,7},{7,0},{8,9},{9,10},{10,1... | collective-permute-start | bytes 147464 | tf_op jit(solution)/shard_map/ppermute | solution.py:20
  102.9 3.9 %collective-permute-start.4 = (f32[6,8,2,128]{3,0,2,1:T(8,128)S(1)}, f32[6,8,2,128]{3,0,2,1:T(8,128)S(1)}, u32[]{:S(2)}, u32[]{:S(2)}) collective-permute-start(f32[6,8,2,128]{3,0,2,1:T(8,128)S(1)} %get-tuple-element.11), channel_id=1, source_target_pairs={{1,0},{2,1},{3,2},{4,3},{5,4},{6,5},{7,6},{0,7},{9,8},{10,9},{11,1... | collective-permute-start | bytes 147464 | tf_op jit(solution)/shard_map/ppermute | solution.py:21
  119.0 50.3 %copy-start.4 = (f32[1,6,8,16,128]{4,3,2,1,0:T(8,128)S(1)}, f32[1,6,8,16,128]{4,3,2,1,0:T(8,128)}, u32[]{:S(2)}) copy-start(f32[1,6,8,16,128]{4,3,2,1,0:T(8,128)} %param.8) | copy-start | bytes 1179652
where the time goes:
time: 174 us; the launch traced here: 173 us
  other arithmetic  67.1 us (39%)
  waiting for transfers between devices  64.3 us (37%)
  starting transfers between devices  16.1 us (9%)
  between operations  11.5 us (7%)
  local copies, waits for them, and re-layouts  10.1 us (6%)
  matrix products  3.79 us (2%)
    ppermute x3, waiting for transfers between devices, padded_2(): before = lax.ppermute(last, axis, up)  63.7 us
    reduce_sum x1, other arithmetic, per_device(): total = jnp.sum(ensemble.astype(jnp.float32) * smoothed, axis=0)  50.3 us
    concatenate x1, other arithmetic, padded_2(): array = jnp.concatenate([before, array, after], axis=dim)  10.7 us
    ppermute x3, starting transfers between devices, padded_2(): after = lax.ppermute(leading, axis, down)  9.6 us
    convert_element_type x1, other arithmetic, per_device(): (ensemble.astype(jnp.float32) * lagrange[None]).astype(jnp.bfloat16)  5.38 us
    slice x2, local copies, waits for them, and re-layouts, padded_2(): last = lax.slice_in_dim(array, length - width, length, axis=dim)  4.07 us
    ppermute x1, starting transfers between devices, passed_along(): return lax.ppermute(block, axis, route)  3.93 us
    dot_general x2, matrix products, tangent_step(): jnp.einsum('lvw,wlxy->vlxy', coupling, center, precision=lax.Precision.HI...  3.79 us
  transfers between devices with their start and end apart: 7, of which 4 were waited for; matrix products, arithmetic and copies ran while one was open for 2% of the time, Pallas kernels for 0%

commit v1 on v0

v1 whole, which is shorter than its diff:
```python
import functools

import jax
import jax.numpy as jnp
from jax import lax
from jax.experimental import pallas as pl
from jax.experimental.pallas import tpu as pltpu
from jax.sharding import PartitionSpec as P


BAND = 128
SPLIT = 2
TILE = 8
GRANT = 16 * 1024 * 1024


def ring(axis, distance):
    size = lax.axis_size(axis)
    return [(i, (i + distance) % size) for i in range(size)]


def divisor(number, limit):
    while number % limit:
        limit -= 1
    return limit


def weights_kernel(span, offsets_ref, out_ref):
    size = out_ref.shape[1]
    row = lax.broadcasted_iota(jnp.int32, (size, size), 0)
    col = lax.broadcasted_iota(jnp.int32, (size, size), 1)
    shift = col - row
    half = span // 2
    same_block = (row // span) == (col // span)
    count = jnp.zeros((size, size), jnp.float32)
    for j in range(offsets_ref.shape[0]):
        count = count + jnp.where(shift == offsets_ref[j], 1.0, 0.0)
    scaled = shift.astype(jnp.float32) * (1.0 / half)
    weight = jnp.where(same_block, count * jnp.exp(-0.5 * scaled * scaled), 0.0)
    across = jnp.where((row // half) != (col // half), weight, 0.0)
    for k, matrix in enumerate((weight, across)):
        high = matrix.astype(jnp.bfloat16)
        out_ref[k, :, :size] = high
        out_ref[k, :, size:] = (matrix - high.astype(jnp.float32)).astype(jnp.bfloat16)


def band_weights(loc_offsets, span, size):
    return pl.pallas_call(
        functools.partial(weights_kernel, span),
        out_shape=jax.ShapeDtypeStruct((2, size, 2 * size), jnp.bfloat16),
        in_specs=[pl.BlockSpec(memory_space=pltpu.SMEM)],
        out_specs=pl.BlockSpec(memory_space=pltpu.VMEM),
        name="weights",
    )(loc_offsets)


def shapes_of_matmul(members, rows):
    stacked = divisor(members, max(1, BAND // rows))
    beside = divisor(members // stacked, 2)
    return stacked, beside


def smoothed_pairs(weights, fields, lam):
    rows, ty = lam.shape
    products = [
        jnp.concatenate([(field * lam).astype(jnp.bfloat16) for field in column], axis=0)
        for column in fields
    ]
    products = jnp.concatenate(products, axis=1)
    smooth = jnp.dot(
        weights, jnp.concatenate([products, products], axis=0), preferred_element_type=jnp.float32
    )
    total = None
    for b, column in enumerate(fields):
        for s, field in enumerate(column):
            pair = field * smooth[s * rows : (s + 1) * rows, b * ty : (b + 1) * ty]
            total = pair if total is None else total + pair
    return total


def interior_kernel(stacked, beside, w_ref, m_ref, lam_ref, out_ref):
    members, nv = m_ref.shape[:2]
    weights = w_ref[0]
    step = stacked * beside

    def variable(v, carry):
        lam = lam_ref[v]
        total = jnp.zeros(lam.shape, jnp.float32)
        for first in range(0, members, step):
            fields = [
                [m_ref[first + b * stacked + s, v].astype(jnp.float32) for s in range(stacked)]
                for b in range(beside)
            ]
            total = total + smoothed_pairs(weights, fields, lam)
        out_ref[v] = total
        return carry

    lax.fori_loop(0, nv, variable, 0)


def vmem():
    return pl.BlockSpec(memory_space=pltpu.VMEM)


def interior(weights, ensemble, lagrange):
    members, nv, rows, ty = ensemble.shape
    stacked, beside = shapes_of_matmul(members, rows)
    return pl.pallas_call(
        functools.partial(interior_kernel, stacked, beside),
        out_shape=jax.ShapeDtypeStruct((nv, rows, ty), jnp.float32),
        in_specs=[vmem()] * 3,
        out_specs=vmem(),
        compiler_params=pltpu.CompilerParams(vmem_limit_bytes=GRANT),
        cost_estimate=pl.CostEstimate(flops=30_000_000_000, bytes_accessed=2 * ensemble.size, transcendentals=0),
        name="interior",
    )(weights, ensemble, lagrange)


def joined(first, second):
    levels, half, ty = first.shape
    both = jnp.concatenate([first[:, None], second[:, None]], axis=1)
    return both.reshape(levels * 2 * half, ty)


def across_kernel(stacked, beside, first_unit, w_ref, up_ref, dn_ref, m_ref, lam_ref, own_a, ret_a, own_b, ret_b):
    members, nv = m_ref.shape[:2]
    number, levels, half, ty = own_a.shape
    span = 2 * half
    pairs = nv // 2
    weights = w_ref[1]

    def unit(u, carry):
        v = (first_unit + u) // SPLIT
        row = (first_unit + u) % SPLIT * levels * span
        rows = pl.ds(pl.multiple_of(row, levels * span), levels * span)

        def halo(ref, index):
            return ref[u, index].astype(jnp.float32)

        def own(block, side):
            block = block.astype(jnp.float32).reshape(levels, 2, half, ty)
            return block[:, side]

        lam_a = joined(halo(up_ref, members), own(lam_ref[v, rows], 0))
        lam_b = joined(own(lam_ref[pairs + v, rows], 1), halo(dn_ref, members))
        total_a = jnp.zeros(lam_a.shape, jnp.float32)
        total_b = jnp.zeros(lam_b.shape, jnp.float32)
        for first in range(0, members, stacked * beside):
            indices = [[first + b * stacked + s for s in range(stacked)] for b in range(beside)]
            fields = [[joined(halo(up_ref, m), own(m_ref[m, v, rows], 0)) for m in column] for column in indices]
            total_a = total_a + smoothed_pairs(weights, fields, lam_a)
            fields = [[joined(own(m_ref[m, pairs + v, rows], 1), halo(dn_ref, m)) for m in column] for column in indices]
            total_b = total_b + smoothed_pairs(weights, fields, lam_b)
        total_a = total_a.reshape(levels, 2, half, ty)
        total_b = total_b.reshape(levels, 2, half, ty)
        ret_a[u] = total_a[:, 0].astype(ret_a.dtype)
        own_a[u] = total_a[:, 1]
        own_b[u] = total_b[:, 0]
        ret_b[u] = total_b[:, 1].astype(ret_b.dtype)
        return carry

    if number == 1:
        unit(0, 0)
    else:
        lax.fori_loop(0, number, unit, 0)


def across(weights, from_left, from_right, ensemble, lagrange, first):
    members, _, _, ty = ensemble.shape
    number, _, levels, half, _ = from_left.shape
    stacked, beside = shapes_of_matmul(members, levels * 2 * half)
    own_type = jax.ShapeDtypeStruct((number, levels, half, ty), jnp.float32)
    ret_type = jax.ShapeDtypeStruct((number, levels, half, ty), jnp.bfloat16)
    return pl.pallas_call(
        functools.partial(across_kernel, stacked, beside, first),
        out_shape=(own_type, ret_type, own_type, ret_type),
        in_specs=[vmem()] * 5,
        out_specs=(vmem(),) * 4,
        compiler_params=pltpu.CompilerParams(vmem_limit_bytes=GRANT),
        cost_estimate=pl.CostEstimate(flops=5_000_000_000 * number, bytes_accessed=ensemble.size // 3, transcendentals=0),
        name="across",
    )(weights, from_left, from_right, ensemble, lagrange)


def pack_kernel(pieces, m_ref, lam_ref, *refs):
    outs, (lam_up, lam_dn, sem) = refs[:-3], refs[-3:]
    members, nv, _, span, _ = m_ref.shape
    half = span // 2
    levels = outs[0].shape[2]
    pairs = nv // 2
    copies = []
    slot = 0
    for piece, (first, number) in enumerate(pieces):
        for u in range(number):
            v, level = (first + u) // SPLIT, (first + u) % SPLIT * levels
            for side, (var, column, lam_buffer) in enumerate(((v, half, lam_up), (pairs + v, 0, lam_dn))):
                out = outs[2 * piece + side]
                at = (pl.ds(level, levels), pl.ds(column, half))
                copies.append(pltpu.make_async_copy(lam_ref.at[(var,) + at], lam_buffer.at[slot], sem.at[len(copies)]))
                copies.append(
                    pltpu.make_async_copy(
                        m_ref.at[(slice(None), var) + at], out.at[u, pl.ds(0, members)], sem.at[len(copies)]
                    )
                )
            slot += 1
    for copy in copies:
        copy.start()
    slot = 0
    for copy in copies[::2]:
        copy.wait()
    for piece, (first, number) in enumerate(pieces):
        for u in range(number):
            for side, lam_buffer in enumerate((lam_up, lam_dn)):
                out = outs[2 * piece + side]
                out[u, members] = lam_buffer[slot].astype(out.dtype)
            slot += 1
    for copy in copies[1::2]:
        copy.wait()


def packed(ensemble, lagrange, pieces):
    members, _, levels, span, ty = ensemble.shape
    half = span // 2
    levels = levels // SPLIT
    types = []
    for _, number in pieces:
        types += [jax.ShapeDtypeStruct((number, members + 1, levels, half, ty), jnp.bfloat16)] * 2
    units = sum(number for _, number in pieces)
    ensemble = pltpu.with_memory_space_constraint(ensemble, pltpu.HBM)
    lagrange = pltpu.with_memory_space_constraint(lagrange, pltpu.HBM)
    hbm = pl.BlockSpec(memory_space=pltpu.HBM)
    return pl.pallas_call(
        functools.partial(pack_kernel, pieces),
        out_shape=tuple(types),
        in_specs=[hbm, hbm],
        out_specs=(vmem(),) * len(types),
        scratch_shapes=[
            pltpu.VMEM((units, levels, half, ty), jnp.float32),
            pltpu.VMEM((units, levels, half, ty), jnp.float32),
            pltpu.SemaphoreType.DMA((4 * units,)),
        ],
        compiler_params=pltpu.CompilerParams(vmem_limit_bytes=GRANT),
        name="pack",
    )(ensemble, lagrange)


def propagate_kernel(c_ref, e_ref, left_ref, right_ref, w_ref, var_ref, lam_ref, state_ref, out_ref, field_ref, wind_ref):
    nv, levels, span, ty = e_ref.shape
    rows = span + 2 * TILE
    field_ref[...] = jnp.zeros_like(field_ref)
    wind_ref[...] = jnp.zeros_like(wind_ref)
    lane = lax.broadcasted_iota(jnp.int32, (rows, ty), 1)

    def one_level(level, carry):
        for v in range(nv):
            field_ref[v, TILE - 2 : TILE] = left_ref[level, 2 * v : 2 * v + 2]
            field_ref[v, TILE : TILE + span] = e_ref[v, level]
            field_ref[v, TILE + span : TILE + span + 2] = right_ref[level, 2 * v : 2 * v + 2]
        for d in range(2):
            wind_ref[d, TILE - 1 : TILE] = left_ref[level, 2 * nv + d : 2 * nv + d + 1]
            wind_ref[d, TILE : TILE + span] = w_ref[d, level]
            wind_ref[d, TILE + span : TILE + span + 1] = right_ref[level, 2 * nv + d : 2 * nv + d + 1]
        cx, cy = wind_ref[0], wind_ref[1]
        cx_plus, cx_minus = jnp.maximum(cx, 0.0), jnp.minimum(cx, 0.0)
        cy_plus, cy_minus = jnp.maximum(cy, 0.0), jnp.minimum(cy, 0.0)
        fields = [field_ref[v] for v in range(nv)]
        for _ in range(2):
            results = []
            for v in range(nv):
                f = fields[v]
                west = pltpu.roll(f, 1, 0)
                east = pltpu.roll(f, rows - 1, 0)
                south = jnp.where(lane == 0, 0.0, pltpu.roll(f, 1, 1))
                north = jnp.where(lane == ty - 1, 0.0, pltpu.roll(f, ty - 1, 1))
                moved = cx_plus * (f - west) + cx_minus * (east - f)
                moved = moved + cy_plus * (f - south) + cy_minus * (north - f)
                mixed = c_ref[level, v, 0] * fields[0]
                for w in range(1, nv):
                    mixed = mixed + c_ref[level, v, w] * fields[w]
                results.append(f - moved + mixed)
            fields = results
        for v in range(nv):
            local = 0.5 * var_ref[v, level] * lam_ref[v, level] + state_ref[v, level]
            out_ref[v, level] = local - fields[v][TILE : TILE + span]
        return carry

    lax.fori_loop(0, levels, one_level, 0)


def propagate(coupling, earlier, left, right, winds, variance, lagrange, state):
    nv, _, span, ty = earlier.shape
    rows = span + 2 * TILE
    return pl.pallas_call(
        propagate_kernel,
        out_shape=jax.ShapeDtypeStruct(earlier.shape, jnp.float32),
        in_specs=[pl.BlockSpec(memory_space=pltpu.SMEM)] + [vmem()] * 7,
        out_specs=vmem(),
        scratch_shapes=[pltpu.VMEM((nv, rows, ty), jnp.float32), pltpu.VMEM((2, rows, ty), jnp.float32)],
        compiler_params=pltpu.CompilerParams(vmem_limit_bytes=GRANT),
        cost_estimate=pl.CostEstimate(flops=10_000_000_000, bytes_accessed=20 * earlier.size, transcendentals=0),
        name="propagate",
    )(coupling, earlier, left, right, winds, variance, lagrange, state)


def final_kernel(scale, counts, base_ref, inner_ref, *refs):
    out_ref = refs[-1]
    nv, levels, span, _ = out_ref.shape
    half = span // 2
    pairs = nv // 2
    part = levels // SPLIT
    unit = 0
    for c, number in enumerate(counts):
        own_a, own_b, back_a, back_b = refs[4 * c : 4 * c + 4]
        for u in range(number):
            v, first = unit // SPLIT, (unit % SPLIT) * part
            at = pl.ds(first, part)
            for var, low, high in (
                (v, own_a[u], back_a[u].astype(jnp.float32)),
                (pairs + v, back_b[u].astype(jnp.float32), own_b[u]),
            ):
                out_ref[var, at, :half] = base_ref[var, at, :half] + scale * (inner_ref[var, at, :half] + low)
                out_ref[var, at, half:] = base_ref[var, at, half:] + scale * (inner_ref[var, at, half:] + high)
            unit += 1


def final(scale, counts, base, inner, parts):
    return pl.pallas_call(
        functools.partial(final_kernel, scale, counts),
        out_shape=jax.ShapeDtypeStruct(base.shape, jnp.float32),
        in_specs=[vmem()] * (2 + len(parts)),
        out_specs=vmem(),
        compiler_params=pltpu.CompilerParams(vmem_limit_bytes=GRANT),
        name="final",
    )(base, inner, *parts)


def per_device(state, multiplier, members, static_var, courant, coupling, loc_offsets):
    own_state = state[0]
    lagrange = multiplier[0]
    ensemble = members[0]
    own_winds = courant[0]
    count, nv, levels, span, ty = ensemble.shape
    rows = levels * span
    flat_members = ensemble.reshape(count, nv, rows, ty)
    flat_lagrange = lagrange.reshape(nv, rows, ty)
    units = nv // 2 * SPLIT
    up, down = ring("space", 1), ring("space", -1)
    later = [(i, i + 1) for i in range(lax.axis_size("tm") - 1)]
    counts = [units // 3, units - units // 3 - units // 6, units // 6]
    firsts = [sum(counts[:c]) for c in range(len(counts))]
    pieces = list(zip(firsts, counts))

    def edges(low):
        take = lambda array, width: array[:, :, :width] if low else array[:, :, span - width :]
        fields = jnp.swapaxes(take(own_state, 2), 0, 1).reshape(levels, 2 * nv, ty)
        winds = jnp.swapaxes(take(own_winds, 1), 0, 1).reshape(levels, 2, ty)
        return jnp.concatenate([fields, winds], axis=1)

    messages = list(packed(ensemble, lagrange, tuple(pieces[:1])))
    messages += packed(ensemble, lagrange, tuple(pieces[1:]))
    from_left = [lax.ppermute(messages[2 * c], "space", up) for c in range(len(pieces))]
    from_right = [lax.ppermute(messages[2 * c + 1], "space", down) for c in range(len(pieces))]
    left = lax.ppermute(edges(False), "space", up)
    right = lax.ppermute(edges(True), "space", down)
    weights = band_weights(loc_offsets, span, max(rows, BAND))
    inner = interior(weights, flat_members, flat_lagrange)
    own_rows = jnp.swapaxes(own_state, 0, 1).reshape(levels, nv * span, ty)
    sent = jnp.concatenate([own_rows, left[:, : 2 * nv], right[:, : 2 * nv]], axis=1)
    came = lax.ppermute(sent, "tm", later)
    earlier = jnp.swapaxes(came[:, : nv * span].reshape(levels, nv, span, ty), 0, 1)
    edge_left = jnp.concatenate([came[:, nv * span : nv * (span + 2)], left[:, 2 * nv :]], axis=1)
    edge_right = jnp.concatenate([came[:, nv * (span + 2) :], right[:, 2 * nv :]], axis=1)
    base = propagate(coupling, earlier, edge_left, edge_right, own_winds, static_var[0], lagrange, own_state)
    parts = []
    for c in range(len(pieces)):
        own_a, ret_a, own_b, ret_b = across(
            weights, from_left[c], from_right[c], flat_members, flat_lagrange, firsts[c]
        )
        parts += [own_a, own_b, lax.ppermute(ret_a, "space", down), lax.ppermute(ret_b, "space", up)]
    result = final(0.5 / (count - 1), counts, base, inner.reshape(base.shape), parts)
    return result[None]


def solution(mesh):
    return jax.shard_map(
        per_device,
        mesh=mesh,
        in_specs=(
            P("tm", None, None, "space", None),
            P("tm", None, None, "space", None),
            P("tm", None, None, None, "space", None),
            P("tm", None, None, "space", None),
            P("tm", None, None, "space", None),
            P(),
            P(),
        ),
        out_specs=P("tm", None, None, "space", None),
        check_vma=False,
    )
```

time: 174 us -> 73.8 us (0.42)
  other arithmetic: 67.1 us -> 2.18 us
  waiting for transfers between devices: 64.3 us -> 17.5 us
  Pallas kernels: 0 us -> 19.5 us
  between operations: 11.5 us -> 0.3 us
  starting transfers between devices: 16.1 us -> 26 us
  matrix products: 3.79 us -> 0 us
  local copies, waits for them, and re-layouts: 10.1 us -> 7.76 us
    reduce_sum x1 -> x0, other arithmetic: 50.3 us -> none  [per_device(): total = jnp.sum(ensemble.astype(jnp.float32) * smoothed, axis=0)]
    ppermute x7 -> x15, waiting for transfers between devices: 64.3 us -> 17.5 us  [the longest x3 15.1 us: per_device(): lax.ppermute(messages[2 * c], 'space', up)]
    pallas_call x0 -> x9, Pallas kernels: none -> 19.5 us  [the longest x3 5.86 us: across(): pl.pallas_call(functools.partial(across_kernel, stacked, beside, first),...]
    ppermute x7 -> x15, starting transfers between devices: 16.1 us -> 26 us  [the longest x3 10.7 us: per_device(): lax.ppermute(messages[2 * c + 1], 'space', down)]
    concatenate x1 -> x4, other arithmetic: 10.7 us -> 2.18 us  [the longest x2 1.28 us: edges(): return jnp.concatenate([fields, winds], axis=1)]
    convert_element_type x3 -> x0, other arithmetic: 5.43 us -> none  [the longest x1 5.38 us: per_device(): (ensemble.astype(jnp.float32) * lagrange[None]).astype(jnp.bfloat16)]
    slice x7 -> x5, local copies, waits for them, and re-layouts: 5.88 us -> 1.69 us  [the longest x1 0.88 us: edges(): array[:, :, span - width:]]
    dot_general x2 -> x0, matrix products: 3.79 us -> none  [tangent_step(): jnp.einsum('lvw,wlxy->vlxy', coupling, center, precision=lax.Precision.HI...]
  transfers between devices with their start and end apart: 7 -> 15, of which waited for: 4 -> 3; matrix products, arithmetic and copies ran while one was open for 2% -> 3% of each run, Pallas kernels for 0% -> 25%
where the time goes in v1:
time: 73.8 us; the launch traced here: 73.3 us
  starting transfers between devices  26 us (35%)
  Pallas kernels  19.5 us (26%)
  waiting for transfers between devices  17.5 us (24%)
  local copies, waits for them, and re-layouts  7.76 us (11%)
  other arithmetic  2.18 us (3%)
    ppermute x3, waiting for transfers between devices, per_device(): lax.ppermute(messages[2 * c], 'space', up)  15.1 us
    ppermute x3, starting transfers between devices, per_device(): lax.ppermute(messages[2 * c + 1], 'space', down)  10.7 us
    ppermute x3, starting transfers between devices, per_device(): lax.ppermute(ret_a, 'space', down)  6.75 us
    pallas_call x3, Pallas kernels, across(): pl.pallas_call(functools.partial(across_kernel, stacked, beside, first),...  5.86 us
    pallas_call x2, Pallas kernels, packed(): pl.pallas_call(functools.partial(pack_kernel, pieces), out_shape=tuple(ty...  5.2 us
    unnamed x17, local copies, waits for them, and re-layouts  4.9 us
    ppermute x1, starting transfers between devices, per_device(): right = lax.ppermute(edges(True), 'space', down)  4.52 us
    pallas_call x1, Pallas kernels, interior(): pl.pallas_call(functools.partial(interior_kernel, stacked, beside), out_s...  3.55 us
  transfers between devices with their start and end apart: 15, of which 3 were waited for; matrix products, arithmetic and copies ran while one was open for 3% of the time, Pallas kernels for 25%

profile of v1, /device:TPU:0, one launch (start us, length us, event | category | flops | bytes accessed | tf_op | source)
XLA Modules:
  0.0 73.3 jit_solution(18265082212500056645)
XLA Ops:
  0.0 0.9 %fusion.1 = (f32[2,8,1,128]{3,2,1,0:T(1,128)S(1)}, f32[2,8,1,128]{3,2,1,0:T(1,128)S(1)}) fusion(f32[2,8,16,128]{3,2,1,0:T(8,128)} %bitcast.48), kind=kLoop, calls=%fused_computation.9 | loop fusion | bytes 32768 | tf_op jit(solution)/shard_map/slice | solution.py:354
  0.9 1.1 %slice_bitcast_fusion.1 = (f32[8,6,2,128]{3,2,0,1:T(2,128)S(1)}, f32[8,6,2,128]{3,2,0,1:T(2,128)S(1)}) fusion(f32[6,8,16,128]{3,2,1,0:T(8,128)} %bitcast.43), kind=kLoop, calls=%fused_computation.7 | loop fusion | bytes 196608 | tf_op jit(solution)/shard_map/transpose | solution.py:355
  2.0 0.6 pad_maximum_fusion.2
  2.6 4.5 %collective-permute-start.1 = (f32[8,14,128]{2,1,0:T(8,128)}, f32[8,14,128]{2,1,0:T(8,128)S(1)}, u32[]{:S(2)}, u32[]{:S(2)}) collective-permute-start(f32[8,14,128]{2,1,0:T(8,128)} %pad_maximum_fusion.2), channel_id=1, source_target_pairs={{0,7},{1,0},{2,1},{3,2},{4,3},{5,4},{6,5},{7,6},{8,15},{9,8},{10,9... | collective-permute-start | bytes 172040 | tf_op jit(solution)/shard_map/ppermute | solution.py:364
  7.2 0.6 pad_maximum_fusion.1
  7.8 2.6 %pack.2 = (bf16[2,41,4,8,128]{4,3,2,1,0:T(8,128)(2,1)}, bf16[2,41,4,8,128]{4,3,2,1,0:T(8,128)(2,1)}) custom-call(bf16[40,6,8,16,128]{4,3,2,1,0:T(8,128)(2,1)} %bitcast.30, f32[6,8,16,128]{3,2,1,0:T(8,128)} %bitcast.36), custom_call_target="tpu_custom_call" | custom-call | tf_op jit(solution)/shard_map/pack/pallas_call | solution.py:232
  10.4 0.1 collective-permute-start.3
  10.5 3.6 %collective-permute-start.4 = (bf16[2,41,4,8,128]{4,3,2,1,0:T(8,128)(2,1)}, bf16[2,41,4,8,128]{4,3,2,1,0:T(8,128)(2,1)}, u32[]{:S(2)}, u32[]{:S(2)}) collective-permute-start(bf16[2,41,4,8,128]{4,3,2,1,0:T(8,128)(2,1)} %get-tuple-element.24), channel_id=1, source_target_pairs={{0,7},{1,0},{2,1},{3,2},{4,3},{5,4},{6,5},{7,6},{8,15},{9,8},{10,9... | collective-permute-start | bytes 2015240 | tf_op jit(solution)/shard_map/ppermute | solution.py:362
  14.1 2.6 %pack.3 = (bf16[3,41,4,8,128]{4,3,2,1,0:T(8,128)(2,1)S(1)}, bf16[3,41,4,8,128]{4,3,2,1,0:T(8,128)(2,1)S(1)}, bf16[1,41,4,8,128]{4,3,2,1,0:T(8,128)(2,1)}, bf16[1,41,4,8,128]{4,3,2,1,0:T(8,128)(2,1)S(1)}) custom-call(bf16[40,6,8,16,128]{4,3,2,1,0:T(8,128)(2,1)} %bitcast.31, f32[6,8,16,128]{3,2,1,0:T(8,128)} %bitcast.37), custom_call_target="tpu_custom_call" | custom-call | tf_op jit(solution)/shard_map/pack/pallas_call | solution.py:232
  16.7 0.7 %copy-done.6 = bf16[1,41,4,8,128]{4,3,2,1,0:T(8,128)(2,1)} copy-done((bf16[1,41,4,8,128]{4,3,2,1,0:T(8,128)(2,1)}, bf16[1,41,4,8,128]{4,3,2,1,0:T(8,128)(2,1)S(1)}, u32[]{:S(2)}) %copy-start.6) | copy-done | bytes 335896
  17.5 1.4 %weights.1.w_ref = bf16[2,128,256]{2,1,0:T(8,128)(2,1)} custom-call(s32[9]{0:T(128)} %offsets_ref.1), custom_call_target="tpu_custom_call" | custom-call | tf_op jit(solution)/shard_map/weights/pallas_call | solution.py:48
  18.9 3.6 %collective-permute-start.12 = (bf16[1,41,4,8,128]{4,3,2,1,0:T(8,128)(2,1)}, bf16[1,41,4,8,128]{4,3,2,1,0:T(8,128)(2,1)S(1)}, u32[]{:S(2)}, u32[]{:S(2)}) collective-permute-start(bf16[1,41,4,8,128]{4,3,2,1,0:T(8,128)(2,1)} %copy-done.6), channel_id=1, source_target_pairs={{0,7},{1,0},{2,1},{3,2},{4,3},{5,4},{6,5},{7,6},{8,15},{9,8},{10,9... | collective-permute-start | bytes 1007624 | tf_op jit(solution)/shard_map/ppermute | solution.py:362
  22.5 0.9 %pad_maximum_fusion = f32[8,120,128]{2,1,0:T(8,128)S(1)} fusion(f32[8,12,128]{2,1,0:T(8,128)S(1)} %bitcast.55, f32[8,12,128]{2,1,0:T(8,128)} %bitcast.29, f32[8,96,128]{2,1,0:T(8,128)S(1)} %bitcast.52), kind=kLoop, calls=%fused_computation | loop fusion | flops 245760 | bytes 983040 | tf_op jit(solution)/shard_map/concatenate | solution.py:368
  23.4 3.4 %collective-permute-start.2 = (f32[8,120,128]{2,1,0:T(8,128)S(1)}, f32[8,120,128]{2,1,0:T(8,128)S(1)}, u32[]{:S(2)}, u32[]{:S(2)}) collective-permute-start(f32[8,120,128]{2,1,0:T(8,128)S(1)} %pad_maximum_fusion), channel_id=1, source_target_pairs={{0,8},{8,16},{16,24},{1,9},{9,17},{17,25},{2,10},{10,18},{18,26},{... | collective-permute-start | bytes 1474568 | tf_op jit(solution)/shard_map/ppermute | solution.py:369
  26.9 0.0 copy-start
  26.9 3.2 %copy-done = bf16[1,40,6,8,16,128]{5,4,3,2,1,0:T(8,128)(2,1)S(1)} copy-done((bf16[1,40,6,8,16,128]{5,4,3,2,1,0:T(8,128)(2,1)S(1)}, bf16[1,40,6,8,16,128]{5,4,3,2,1,0:T(8,128)(2,1)}, u32[]{:S(2)}) %copy-start) | copy-done | bytes 7864344
  30.1 0.9 %copy-done.3 = bf16[2,128,256]{2,1,0:T(8,128)(2,1)S(1)} copy-done((bf16[2,128,256]{2,1,0:T(8,128)(2,1)S(1)}, bf16[2,128,256]{2,1,0:T(8,128)(2,1)}, u32[]{:S(2)}) %copy-start.3) | copy-done | bytes 131096
  31.0 3.5 %interior.1 = f32[6,128,128]{2,1,0:T(8,128)S(1)} custom-call(bf16[2,128,256]{2,1,0:T(8,128)(2,1)S(1)} %copy-done.3, bf16[40,6,128,128]{3,2,1,0:T(8,128)(2,1)S(1)} %bitcast.32, f32[6,128,128]{2,1,0:T(8,128)S(1)} %bitcast.38), custom_call_target="tpu_custom_call" | custom-call | flops 30000001024 | bytes 7864320 | tf_op jit(solution)/shard_map/interior/pallas_call | solution.py:108
  34.6 0.8 %slice.52 = f32[8,2,128]{2,1,0:T(2,128)S(1)} slice(f32[8,14,128]{2,1,0:T(8,128)} %collective-permute-done), slice={[0:8], [12:14], [0:128]} | slice | bytes 16384 | tf_op jit(solution)/shard_map/slice | solution.py:371
  35.4 1.1 %collective-permute-done.11.up_ref = bf16[1,41,4,8,128]{4,3,2,1,0:T(8,128)(2,1)} collective-permute-done((bf16[1,41,4,8,128]{4,3,2,1,0:T(8,128)(2,1)}, bf16[1,41,4,8,128]{4,3,2,1,0:T(8,128)(2,1)}, u32[]{:S(2)}, u32[]{:S(2)}) %collective-permute-start.11) | collective-permute-done | bytes 335904 | tf_op jit(solution)/shard_map/ppermute | solution.py:361
  36.5 3.5 %collective-permute-start.8 = (bf16[3,41,4,8,128]{4,3,2,1,0:T(8,128)(2,1)S(1)}, bf16[3,41,4,8,128]{4,3,2,1,0:T(8,128)(2,1)S(1)}, u32[]{:S(2)}, u32[]{:S(2)}) collective-permute-start(bf16[3,41,4,8,128]{4,3,2,1,0:T(8,128)(2,1)S(1)} %get-tuple-element.30), channel_id=1, source_target_pairs={{0,7},{1,0},{2,1},{3,2},{4,3},{5,4},{6,5},{7,6},{8,15},{9,8},{10,9... | collective-permute-start | bytes 3022856 | tf_op jit(solution)/shard_map/ppermute | solution.py:362
  40.0 1.6 %across.5 = (f32[1,4,8,128]{3,2,1,0:T(8,128)S(1)}, bf16[1,4,8,128]{3,2,1,0:T(8,128)(2,1)S(1)}, f32[1,4,8,128]{3,2,1,0:T(8,128)S(1)}, bf16[1,4,8,128]{3,2,1,0:T(8,128)(2,1)S(1)}) custom-call(bf16[2,128,256]{2,1,0:T(8,128)(2,1)S(1)} %copy-done.3, bf16[1,41,4,8,128]{4,3,2,1,0:T(8,128)(2,1)} %collective-permute-done.11.up_ref, ...), custom_call_target="tpu_custom_call" | custom-call | flops 5000000000 | bytes 1310720 | tf_op jit(solution)/shard_map/across/pallas_call | solution.py:174
  41.6 0.1 collective-permute-start.13
  41.8 0.5 collective-permute-start.14
  42.4 2.4 %across.3 = (f32[2,4,8,128]{3,2,1,0:T(8,128)S(1)}, bf16[2,4,8,128]{3,2,1,0:T(8,128)(2,1)S(1)}, f32[2,4,8,128]{3,2,1,0:T(8,128)S(1)}, bf16[2,4,8,128]{3,2,1,0:T(8,128)(2,1)S(1)}) custom-call(bf16[2,128,256]{2,1,0:T(8,128)(2,1)S(1)} %copy-done.3, bf16[2,41,4,8,128]{4,3,2,1,0:T(8,128)(2,1)S(1)} %collective-permute-done.3.up_ref, ...), custom_call_target="tpu_custom_call" | custom-call | flops 10000000000 | bytes 1310720 | tf_op jit(solution)/shard_map/across/pallas_call | solution.py:174
  44.8 3.1 %collective-permute-start.5 = (bf16[2,4,8,128]{3,2,1,0:T(8,128)(2,1)S(1)}, bf16[2,4,8,128]{3,2,1,0:T(8,128)(2,1)S(1)}, u32[]{:S(2)}, u32[]{:S(2)}) collective-permute-start(bf16[2,4,8,128]{3,2,1,0:T(8,128)(2,1)S(1)} %get-tuple-element.27), channel_id=1, source_target_pairs={{0,7},{1,0},{2,1},{3,2},{4,3},{5,4},{6,5},{7,6},{8,15},{9,8},{10,9... | collective-permute-start | bytes 49160 | tf_op jit(solution)/shard_map/ppermute | solution.py:379
  47.9 14.0 %collective-permute-done.7.up_ref = bf16[3,41,4,8,128]{4,3,2,1,0:T(8,128)(2,1)S(1)} collective-permute-done((bf16[3,41,4,8,128]{4,3,2,1,0:T(8,128)(2,1)S(1)}, bf16[3,41,4,8,128]{4,3,2,1,0:T(8,128)(2,1)S(1)}, u32[]{:S(2)}, u32[]{:S(2)}) %collective-permute-start.7) | collective-permute-done | bytes 1007648 | tf_op jit(solution)/shard_map/ppermute | solution.py:361
  61.9 1.9 %across.4 = (f32[3,4,8,128]{3,2,1,0:T(8,128)S(1)}, bf16[3,4,8,128]{3,2,1,0:T(8,128)(2,1)S(1)}, f32[3,4,8,128]{3,2,1,0:T(8,128)S(1)}, bf16[3,4,8,128]{3,2,1,0:T(8,128)(2,1)S(1)}) custom-call(bf16[2,128,256]{2,1,0:T(8,128)(2,1)S(1)} %copy-done.3, bf16[3,41,4,8,128]{4,3,2,1,0:T(8,128)(2,1)S(1)} %collective-permute-done.7.up_ref, ...), custom_call_target="tpu_custom_call" | custom-call | flops 15000000512 | bytes 1310720 | tf_op jit(solution)/shard_map/across/pallas_call | solution.py:174
  63.8 3.6 %collective-permute-start.9 = (bf16[3,4,8,128]{3,2,1,0:T(8,128)(2,1)S(1)}, bf16[3,4,8,128]{3,2,1,0:T(8,128)(2,1)S(1)}, u32[]{:S(2)}, u32[]{:S(2)}) collective-permute-start(bf16[3,4,8,128]{3,2,1,0:T(8,128)(2,1)S(1)} %get-tuple-element.33), channel_id=1, source_target_pairs={{0,7},{1,0},{2,1},{3,2},{4,3},{5,4},{6,5},{7,6},{8,15},{9,8},{10,9... | collective-permute-start | bytes 73736 | tf_op jit(solution)/shard_map/ppermute | solution.py:379
  67.4 2.6 %propagate.1.base_ref = f32[6,8,16,128]{3,2,1,0:T(8,128)S(1)} custom-call(f32[8,6,6]{2,1,0:T(8,128)S(1)} %copy.20.c_ref, f32[6,8,16,128]{3,2,1,0:T(8,128)S(1)} %bitcast.46, f32[8,14,128]{2,1,0:T(8,128)S(1)} %get-tuple-element.47.left_ref, f32[8,14,128]{2,1,0:T(8,128)S(1)} %get-tuple-element.48.right_ref, f32[2,8,16,128]{3,2,1,0:T(8,128)S(1)} %bitcast.49, ...), custom_call_target="tpu_custom_call" | custom-call | flops 10000000000 | bytes 1966080 | tf_op jit(solution)/shard_map/propagate/pallas_call | solution.py:293
  70.1 2.3 %collective-permute-done.10.refs_7_ = bf16[3,4,8,128]{3,2,1,0:T(8,128)(2,1)S(1)} collective-permute-done((bf16[3,4,8,128]{3,2,1,0:T(8,128)(2,1)S(1)}, bf16[3,4,8,128]{3,2,1,0:T(8,128)(2,1)S(1)}, u32[]{:S(2)}, u32[]{:S(2)}) %collective-permute-start.10) | collective-permute-done | bytes 24608 | tf_op jit(solution)/shard_map/ppermute | solution.py:379
  72.5 0.8 %final.1 = f32[6,8,16,128]{3,2,1,0:T(8,128)} custom-call(f32[6,8,16,128]{3,2,1,0:T(8,128)S(1)} %propagate.1.base_ref, f32[6,8,16,128]{3,2,1,0:T(8,128)S(1)} %bitcast.47, f32[2,4,8,128]{3,2,1,0:T(8,128)S(1)} %get-tuple-element.25.refs_0_, f32[2,4,8,128]{3,2,1,0:T(8,128)S(1)} %get-tuple-element.26.refs_1_, ...), custom_call_target="tpu_custom_call" | custom-call | tf_op jit(solution)/shard_map/final/pallas_call | solution.py:327
  (42 shorter events, 0.2 us)
Async XLA Ops:
  2.6 16.3 %collective-permute-start.1 = (f32[8,14,128]{2,1,0:T(8,128)}, f32[8,14,128]{2,1,0:T(8,128)S(1)}, u32[]{:S(2)}, u32[]{:S(2)}) collective-permute-start(f32[8,14,128]{2,1,0:T(8,128)} %pad_maximum_fusion.2), channel_id=1, source_target_pairs={{0,7},{1,0},{2,1},{3,2},{4,3},{5,4},{6,5},{7,6},{8,15},{9,8},{10,9... | collective-permute-start | bytes 172040 | tf_op jit(solution)/shard_map/ppermute | solution.py:364
  7.8 14.7 %collective-permute-start = (f32[8,14,128]{2,1,0:T(8,128)}, f32[8,14,128]{2,1,0:T(8,128)}, u32[]{:S(2)}, u32[]{:S(2)}) collective-permute-start(f32[8,14,128]{2,1,0:T(8,128)} %pad_maximum_fusion.1), channel_id=1, source_target_pairs={{0,1},{1,2},{2,3},{3,4},{4,5},{5,6},{6,7},{7,0},{8,9},{9,10},{10,1... | collective-permute-start | bytes 172040 | tf_op jit(solution)/shard_map/ppermute | solution.py:363
  7.8 11.1 %copy-start.2 = (f32[1,6,8,16,128]{4,3,2,1,0:T(8,128)S(1)}, f32[1,6,8,16,128]{4,3,2,1,0:T(8,128)}, u32[]{:S(2)}) copy-start(f32[1,6,8,16,128]{4,3,2,1,0:T(8,128)} %param.7) | copy-start | bytes 1179652
  7.8 19.0 %copy-start.1 = (f32[1,6,8,16,128]{4,3,2,1,0:T(8,128)S(1)}, f32[1,6,8,16,128]{4,3,2,1,0:T(8,128)}, u32[]{:S(2)}) copy-start(f32[1,6,8,16,128]{4,3,2,1,0:T(8,128)} %param.8) | copy-start | bytes 1179652
  10.4 31.4 %collective-permute-start.3 = (bf16[2,41,4,8,128]{4,3,2,1,0:T(8,128)(2,1)}, bf16[2,41,4,8,128]{4,3,2,1,0:T(8,128)(2,1)S(1)}, u32[]{:S(2)}, u32[]{:S(2)}) collective-permute-start(bf16[2,41,4,8,128]{4,3,2,1,0:T(8,128)(2,1)} %get-tuple-element.23), channel_id=1, source_target_pairs={{0,1},{1,2},{2,3},{3,4},{4,5},{5,6},{6,7},{7,0},{8,9},{9,10},{10,1... | collective-permute-start | bytes 2015240 | tf_op jit(solution)/shard_map/ppermute | solution.py:361
  10.5 31.9 %collective-permute-start.4 = (bf16[2,41,4,8,128]{4,3,2,1,0:T(8,128)(2,1)}, bf16[2,41,4,8,128]{4,3,2,1,0:T(8,128)(2,1)}, u32[]{:S(2)}, u32[]{:S(2)}) collective-permute-start(bf16[2,41,4,8,128]{4,3,2,1,0:T(8,128)(2,1)} %get-tuple-element.24), channel_id=1, source_target_pairs={{0,7},{1,0},{2,1},{3,2},{4,3},{5,4},{6,5},{7,6},{8,15},{9,8},{10,9... | collective-permute-start | bytes 2015240 | tf_op jit(solution)/shard_map/ppermute | solution.py:362
  16.7 0.8 %copy-start.6 = (bf16[1,41,4,8,128]{4,3,2,1,0:T(8,128)(2,1)}, bf16[1,41,4,8,128]{4,3,2,1,0:T(8,128)(2,1)S(1)}, u32[]{:S(2)}) copy-start(bf16[1,41,4,8,128]{4,3,2,1,0:T(8,128)(2,1)S(1)} %get-tuple-element.36) | copy-start | bytes 1007620
  17.5 19.0 %collective-permute-start.11 = (bf16[1,41,4,8,128]{4,3,2,1,0:T(8,128)(2,1)}, bf16[1,41,4,8,128]{4,3,2,1,0:T(8,128)(2,1)}, u32[]{:S(2)}, u32[]{:S(2)}) collective-permute-start(bf16[1,41,4,8,128]{4,3,2,1,0:T(8,128)(2,1)} %get-tuple-element.35), channel_id=1, source_target_pairs={{0,1},{1,2},{2,3},{3,4},{4,5},{5,6},{6,7},{7,0},{8,9},{9,10},{10,1... | collective-permute-start | bytes 1007624 | tf_op jit(solution)/shard_map/ppermute | solution.py:361
  18.9 17.5 %collective-permute-start.12 = (bf16[1,41,4,8,128]{4,3,2,1,0:T(8,128)(2,1)}, bf16[1,41,4,8,128]{4,3,2,1,0:T(8,128)(2,1)S(1)}, u32[]{:S(2)}, u32[]{:S(2)}) collective-permute-start(bf16[1,41,4,8,128]{4,3,2,1,0:T(8,128)(2,1)} %copy-done.6), channel_id=1, source_target_pairs={{0,7},{1,0},{2,1},{3,2},{4,3},{5,4},{6,5},{7,6},{8,15},{9,8},{10,9... | collective-permute-start | bytes 1007624 | tf_op jit(solution)/shard_map/ppermute | solution.py:362
  23.4 18.2 %collective-permute-start.2 = (f32[8,120,128]{2,1,0:T(8,128)S(1)}, f32[8,120,128]{2,1,0:T(8,128)S(1)}, u32[]{:S(2)}, u32[]{:S(2)}) collective-permute-start(f32[8,120,128]{2,1,0:T(8,128)S(1)} %pad_maximum_fusion), channel_id=1, source_target_pairs={{0,8},{8,16},{16,24},{1,9},{9,17},{17,25},{2,10},{10,18},{18,26},{... | collective-permute-start | bytes 1474568 | tf_op jit(solution)/shard_map/ppermute | solution.py:369
  26.9 3.2 %copy-start = (bf16[1,40,6,8,16,128]{5,4,3,2,1,0:T(8,128)(2,1)S(1)}, bf16[1,40,6,8,16,128]{5,4,3,2,1,0:T(8,128)(2,1)}, u32[]{:S(2)}) copy-start(bf16[1,40,6,8,16,128]{5,4,3,2,1,0:T(8,128)(2,1)} %param.9) | copy-start | bytes 23592964
  30.1 0.9 %copy-start.3 = (bf16[2,128,256]{2,1,0:T(8,128)(2,1)S(1)}, bf16[2,128,256]{2,1,0:T(8,128)(2,1)}, u32[]{:S(2)}) copy-start(bf16[2,128,256]{2,1,0:T(8,128)(2,1)} %weights.1.w_ref) | copy-start | bytes 393220
  31.0 3.6 %copy-start.7 = (f32[8,6,6]{2,0,1:T(8,128)S(1)}, f32[8,6,6]{2,0,1:T(8,128)}, u32[]{:S(2)}) copy-start(f32[8,6,6]{2,0,1:T(8,128)} %param.12) | copy-start | bytes 3460
  36.5 25.4 %collective-permute-start.7 = (bf16[3,41,4,8,128]{4,3,2,1,0:T(8,128)(2,1)S(1)}, bf16[3,41,4,8,128]{4,3,2,1,0:T(8,128)(2,1)S(1)}, u32[]{:S(2)}, u32[]{:S(2)}) collective-permute-start(bf16[3,41,4,8,128]{4,3,2,1,0:T(8,128)(2,1)S(1)} %get-tuple-element.29), channel_id=1, source_target_pairs={{0,1},{1,2},{2,3},{3,4},{4,5},{5,6},{6,7},{7,0},{8,9},{9,10},{10,1... | collective-permute-start | bytes 3022856 | tf_op jit(solution)/shard_map/ppermute | solution.py:361
  36.5 25.4 %collective-permute-start.8 = (bf16[3,41,4,8,128]{4,3,2,1,0:T(8,128)(2,1)S(1)}, bf16[3,41,4,8,128]{4,3,2,1,0:T(8,128)(2,1)S(1)}, u32[]{:S(2)}, u32[]{:S(2)}) collective-permute-start(bf16[3,41,4,8,128]{4,3,2,1,0:T(8,128)(2,1)S(1)} %get-tuple-element.30), channel_id=1, source_target_pairs={{0,7},{1,0},{2,1},{3,2},{4,3},{5,4},{6,5},{7,6},{8,15},{9,8},{10,9... | collective-permute-start | bytes 3022856 | tf_op jit(solution)/shard_map/ppermute | solution.py:362
  41.6 25.8 %collective-permute-start.13 = (bf16[1,4,8,128]{3,2,1,0:T(8,128)(2,1)S(1)}, bf16[1,4,8,128]{3,2,1,0:T(8,128)(2,1)S(1)}, u32[]{:S(2)}, u32[]{:S(2)}) collective-permute-start(bf16[1,4,8,128]{3,2,1,0:T(8,128)(2,1)S(1)} %get-tuple-element.39), channel_id=1, source_target_pairs={{0,7},{1,0},{2,1},{3,2},{4,3},{5,4},{6,5},{7,6},{8,15},{9,8},{10,9... | collective-permute-start | bytes 24584 | tf_op jit(solution)/shard_map/ppermute | solution.py:379
  41.8 28.2 %collective-permute-start.14 = (bf16[1,4,8,128]{3,2,1,0:T(8,128)(2,1)S(1)}, bf16[1,4,8,128]{3,2,1,0:T(8,128)(2,1)S(1)}, u32[]{:S(2)}, u32[]{:S(2)}) collective-permute-start(bf16[1,4,8,128]{3,2,1,0:T(8,128)(2,1)S(1)} %get-tuple-element.40), channel_id=1, source_target_pairs={{0,1},{1,2},{2,3},{3,4},{4,5},{5,6},{6,7},{7,0},{8,9},{9,10},{10,1... | collective-permute-start | bytes 24584 | tf_op jit(solution)/shard_map/ppermute | solution.py:379
  44.8 25.3 %collective-permute-start.5 = (bf16[2,4,8,128]{3,2,1,0:T(8,128)(2,1)S(1)}, bf16[2,4,8,128]{3,2,1,0:T(8,128)(2,1)S(1)}, u32[]{:S(2)}, u32[]{:S(2)}) collective-permute-start(bf16[2,4,8,128]{3,2,1,0:T(8,128)(2,1)S(1)} %get-tuple-element.27), channel_id=1, source_target_pairs={{0,7},{1,0},{2,1},{3,2},{4,3},{5,4},{6,5},{7,6},{8,15},{9,8},{10,9... | collective-permute-start | bytes 49160 | tf_op jit(solution)/shard_map/ppermute | solution.py:379
  61.9 5.5 %copy-start.4 = (f32[1,2,8,16,128]{4,3,2,1,0:T(8,128)S(1)}, f32[1,2,8,16,128]{4,3,2,1,0:T(8,128)}, u32[]{:S(2)}) copy-start(f32[1,2,8,16,128]{4,3,2,1,0:T(8,128)} %param.11) | copy-start | bytes 393220
  61.9 5.5 %copy-start.5 = (f32[1,6,8,16,128]{4,3,2,1,0:T(8,128)S(1)}, f32[1,6,8,16,128]{4,3,2,1,0:T(8,128)}, u32[]{:S(2)}) copy-start(f32[1,6,8,16,128]{4,3,2,1,0:T(8,128)} %param.10) | copy-start | bytes 1179652
  61.9 8.2 %collective-permute-start.6 = (bf16[2,4,8,128]{3,2,1,0:T(8,128)(2,1)S(1)}, bf16[2,4,8,128]{3,2,1,0:T(8,128)(2,1)S(1)}, u32[]{:S(2)}, u32[]{:S(2)}) collective-permute-start(bf16[2,4,8,128]{3,2,1,0:T(8,128)(2,1)S(1)} %get-tuple-element.28), channel_id=1, source_target_pairs={{0,1},{1,2},{2,3},{3,4},{4,5},{5,6},{6,7},{7,0},{8,9},{9,10},{10,1... | collective-permute-start | bytes 49160 | tf_op jit(solution)/shard_map/ppermute | solution.py:379
  63.8 6.3 %collective-permute-start.9 = (bf16[3,4,8,128]{3,2,1,0:T(8,128)(2,1)S(1)}, bf16[3,4,8,128]{3,2,1,0:T(8,128)(2,1)S(1)}, u32[]{:S(2)}, u32[]{:S(2)}) collective-permute-start(bf16[3,4,8,128]{3,2,1,0:T(8,128)(2,1)S(1)} %get-tuple-element.33), channel_id=1, source_target_pairs={{0,7},{1,0},{2,1},{3,2},{4,3},{5,4},{6,5},{7,6},{8,15},{9,8},{10,9... | collective-permute-start | bytes 73736 | tf_op jit(solution)/shard_map/ppermute | solution.py:379
  67.4 5.1 %collective-permute-start.10 = (bf16[3,4,8,128]{3,2,1,0:T(8,128)(2,1)S(1)}, bf16[3,4,8,128]{3,2,1,0:T(8,128)(2,1)S(1)}, u32[]{:S(2)}, u32[]{:S(2)}) collective-permute-start(bf16[3,4,8,128]{3,2,1,0:T(8,128)(2,1)S(1)} %get-tuple-element.34), channel_id=1, source_target_pairs={{0,1},{1,2},{2,3},{3,4},{4,5},{5,6},{6,7},{7,0},{8,9},{9,10},{10,1... | collective-permute-start | bytes 73736 | tf_op jit(solution)/shard_map/ppermute | solution.py:379
